TPU v7x, 768 devices: a whole 4x8x12 slice. The times are simulated.
768 devices in a mesh: seq: 96 (over z, x, core), head: 8 (over y).
Axes of the slice: x: 4, y: 8, z: 12, core: 2. Of those that a mesh axis runs over, the one named last changes fastest.
Arguments:
- queries: bfloat16 [49152, 4096], P('seq', 'head'), may hold values from -360 to 360, as said below
- key_rows: bfloat16 [49152, 1024], P('seq', 'head'), may hold values from -6 to 6
- value_rows: bfloat16 [49152, 1024], P('seq', 'head'), may hold values from -6 to 6
- doc_lengths: int32 [96], replicated, may hold values from 1 to 1536, 49152 in all
Outputs:
- attn_out: bfloat16 [49152, 4096], P(('seq', 'head'))
Inputs may be any that keep to these rules, and one draw needn't show every extreme that they name: `queries`: custom draw of bounded query entries. `doc_lengths`: the lengths sum to 49152; each is at most 1536.
All inputs are finite; a program needn't handle non-finite values.
Results may differ from a plain program's by a relative error of at most 0.0036.
Values may be sent and summed in bfloat16 or wider, within the bound.
No kernel may reach another device: no remote copies, remote signals or barrier semaphores. Data moves between devices by JAX's collectives and lax.ppermute only.
A program may use at most 32 MiB of HBM per device.

v0:
```python
import functools

import jax
import jax.numpy as jnp
from jax import lax
from jax.experimental import pallas as pl
from jax.experimental.pallas import tpu as pltpu
from jax.sharding import PartitionSpec as P


HD = 128
GROUP = 4
T = 512
LANES = 128
FAR = 4194304.0
SCALE = 0.08838834764831845 * 1.4426950408889634
QT = 256
HEADS = 4


def inside(docs_ref, base, rows):
    position = base + lax.broadcasted_iota(jnp.int32, (rows, LANES), 0)
    return (position >= docs_ref[0:1, :]) & (position < docs_ref[1:2, :])


def attend(causal, start, last, backs, where_ref, docs_ref, q_ref, *refs):
    refs = list(refs)
    first, odd = where_ref[0], where_ref[1]
    state = None if start else (refs.pop(0), refs.pop(0))
    blocks = [refs.pop(0) for _ in backs]
    if start:
        sem, q_hbm, q_ref = refs.pop(), q_ref, refs.pop(0)
        fetch = pltpu.make_async_copy(q_hbm, q_ref, sem)
        fetch.start()
    kw, vw = refs[-2:]
    outs = refs[:-2]
    for i, (even_back, odd_back) in enumerate(backs):
        rows = slice(i * T, (i + 1) * T)
        base = first - (even_back + odd * (odd_back - even_back)) * T
        kw[rows, :HD] = blocks[i][:T, :]
        kw[rows, HD:] = jnp.where(inside(docs_ref, base, T), 0.0, -FAR).astype(jnp.bfloat16)
        vw[rows, :HD] = blocks[i][T:, :]
        vw[rows, HD:] = jnp.ones((T, HD), jnp.bfloat16)
    below = None
    if causal:
        row = lax.broadcasted_iota(jnp.int32, (HEADS * QT, QT), 0) % QT
        below = lax.broadcasted_iota(jnp.int32, (HEADS * QT, QT), 1) <= row
    owns = [
        jnp.where(inside(docs_ref, first + low, QT), 1.0, 0.0).astype(jnp.bfloat16) for low in range(0, T, QT)
    ]

    def width(unit):
        return unit[0] * QT + QT if causal else len(backs) * T

    def score(unit):
        tile, head = unit
        rows = slice(tile * QT, tile * QT + QT)
        query = jnp.concatenate(
            [
                jnp.concatenate([q_ref[rows, h * HD : (h + 1) * HD], owns[tile]], 1)
                for h in range(head, head + HEADS)
            ],
            0,
        )
        scores = lax.dot_general(
            query, kw[: width(unit), :], (((1,), (1,)), ((), ())), preferred_element_type=jnp.float32
        )
        if causal:
            low = tile * QT
            tail = jnp.where(below, scores[:, low:], -FAR)
            scores = tail if low == 0 else jnp.concatenate([scores[:, :low], tail], 1)
        return scores

    def mix(unit, scores):
        tile, head = unit
        at = (tile * GROUP + head) * QT
        rows = slice(at, at + HEADS * QT)
        largest = jnp.max(scores, axis=1, keepdims=True)
        if start:
            weights = jnp.exp2((scores - largest) * SCALE).astype(jnp.bfloat16)
        else:
            before = state[0][rows, :]
            largest = jnp.maximum(before, largest)
            shrink = jnp.exp2((before - largest) * SCALE)
            weights = jnp.exp2((scores - jnp.concatenate([largest] * (width(unit) // HD), 1)) * SCALE)
            weights = weights.astype(jnp.bfloat16)
        mixed = jnp.dot(weights, vw[: width(unit), :], preferred_element_type=jnp.float32)
        top, total = mixed[:, :HD], mixed[:, HD:]
        if not start:
            top = top + state[1][rows, :HD] * shrink
            total = total + state[1][rows, HD:] * shrink
        if last:
            result = (top / total).astype(jnp.bfloat16)
            for i in range(HEADS):
                columns = slice((head + i) * HD, (head + i + 1) * HD)
                outs[0][tile * QT : tile * QT + QT, columns] = result[i * QT : (i + 1) * QT]
        else:
            outs[0][rows, :] = jnp.broadcast_to(largest, (HEADS * QT, HD))
            outs[1][rows, :HD] = top
            outs[1][rows, HD:] = total

    units = [(tile, head) for tile in range(T // QT) for head in range(0, GROUP, HEADS)]
    if start:
        fetch.wait()
    ahead = score(units[0])
    for i, unit in enumerate(units):
        scores, ahead = ahead, score(units[i + 1]) if i + 1 < len(units) else None
        mix(unit, scores)


STATE = [
    jax.ShapeDtypeStruct((GROUP * T, HD), jnp.float32),
    jax.ShapeDtypeStruct((GROUP * T, 2 * HD), jnp.float32),
]
RESULT = [jax.ShapeDtypeStruct((T, GROUP * HD), jnp.bfloat16)]


def in_hbm(x):
    return pltpu.with_memory_space_constraint(x, pltpu.HBM)


def stage(where, docs, queries, state, blocks, backs, causal=False, last=False):
    vmem = pl.BlockSpec(memory_space=pltpu.VMEM)
    start = not state
    out_shape = RESULT if last else STATE
    scratch = [pltpu.VMEM((len(blocks) * T, 2 * HD), jnp.bfloat16)] * 2
    if start:
        out_shape = [jax.ShapeDtypeStruct(queries.shape, queries.dtype)] + out_shape
        scratch.append(pltpu.SemaphoreType.DMA(()))
    args = (*state, *blocks)
    return pl.pallas_call(
        functools.partial(attend, causal, start, last, backs),
        out_shape=out_shape,
        in_specs=[pl.BlockSpec(memory_space=pltpu.SMEM), vmem, pl.BlockSpec(memory_space=pltpu.HBM) if start else vmem]
        + [vmem] * len(args),
        out_specs=[vmem] * len(out_shape),
        scratch_shapes=scratch,
        compiler_params=pltpu.CompilerParams(vmem_limit_bytes=28 << 20),
        cost_estimate=pl.CostEstimate(
            flops=10**9 * len(blocks), transcendentals=10**6 * len(blocks), bytes_accessed=10**6
        ),
    )(where, docs, in_hbm(queries) if start else queries, *args)


def pack_kernel(k_ref, v_ref, lengths_ref, rows_ref, docs_ref, lengths, sems):
    copies = [
        pltpu.make_async_copy(lengths_ref, lengths, sems.at[0]),
        pltpu.make_async_copy(k_ref, rows_ref.at[:T, :], sems.at[1]),
        pltpu.make_async_copy(v_ref, rows_ref.at[T:, :], sems.at[2]),
    ]
    for copy in copies:
        copy.start()
    copies[0].wait()
    lane = lax.broadcasted_iota(jnp.int32, (1, LANES), 1)
    begins = jnp.full((1, LANES), 1 << 30, jnp.int32)
    ends = begins
    reached = jnp.int32(0)
    for i in range(lengths.shape[0]):
        begins = jnp.where(lane == i, reached, begins)
        reached = reached + lengths[i]
        ends = jnp.where(lane == i, reached, ends)
    docs_ref[0:1, :] = begins
    docs_ref[1:2, :] = ends
    copies[1].wait()
    copies[2].wait()


def pack(keys, values, doc_lengths):
    vmem = pl.BlockSpec(memory_space=pltpu.VMEM)
    return pl.pallas_call(
        pack_kernel,
        out_shape=[pltpu.VMEM((2 * T, HD), jnp.bfloat16), pltpu.VMEM((2, LANES), jnp.int32)],
        in_specs=[pl.BlockSpec(memory_space=pltpu.HBM)] * 3,
        out_specs=[vmem, vmem],
        scratch_shapes=[pltpu.SMEM(doc_lengths.shape, jnp.int32), pltpu.SemaphoreType.DMA((3,))],
        name="pack",
    )(*(in_hbm(x) for x in (keys, values, doc_lengths)))


def per_device(queries, key_rows, value_rows, doc_lengths):
    blocks = lax.axis_size("seq")
    block = lax.axis_index("seq")
    rows, docs = pack(key_rows, value_rows, doc_lengths)
    a = lax.ppermute(rows, "seq", [(i, i + 2) for i in range(blocks - 2)])
    hops = [(i, i + 1 if i % 2 == 0 else i + 3) for i in range(blocks)]
    x = lax.ppermute(rows, "seq", [(i, j) for i, j in hops if j < blocks])
    s = lax.ppermute(a, "seq", [(i, i ^ 1) for i in range(blocks)])
    where = jnp.stack([block * T, block % 2]).astype(jnp.int32)
    near, *state = stage(where, docs, queries, (), (rows,), ((0, 0),), causal=True)
    state = stage(where, docs, near, state, (a,), ((2, 2),))
    (merged,) = stage(where, docs, near, state, (s, x), ((1, 3), (3, 1)), last=True)
    return lax.all_to_all(merged, "head", split_axis=0, concat_axis=1, tiled=True)


def solution(mesh):
    in_specs = (P("seq", "head"), P("seq", "head"), P("seq", "head"), P())
    out_specs = P(("seq", "head"), None)
    return jax.shard_map(per_device, mesh=mesh, in_specs=in_specs, out_specs=out_specs, check_vma=False)
```

profile of v0, /device:TPU:512, one launch (start us, length us, event | category | flops | bytes accessed | tf_op | source)
XLA Modules:
  0.0 52.7 jit_solution(7163260735426098477)
XLA Ops:
  0.0 1.0 %pack.1 = (bf16[1024,128]{1,0:T(8,128)(2,1)S(1)}, s32[2,128]{1,0:T(2,128)S(1)}) custom-call(bf16[512,128]{1,0:T(8,128)(2,1)} %k_ref.1, bf16[512,128]{1,0:T(8,128)(2,1)} %v_ref.1, s32[96]{0:T(128)} %lengths_ref.1), custom_call_target="tpu_custom_call" | custom-call | tf_op jit(solution)/shard_map/pack/pallas_call | solution.py:170
  1.0 3.4 %collective-permute-start = (bf16[1024,128]{1,0:T(8,128)(2,1)S(1)}, bf16[1024,128]{1,0:T(8,128)(2,1)S(1)}, u32[]{:S(2)}, u32[]{:S(2)}) collective-permute-start(bf16[1024,128]{1,0:T(8,128)(2,1)S(1)} %get-tuple-element.13.refs_0_), channel_id=1, source_target_pairs={{0,16},{8,24},{16,32},{24,40},{32,48},{40,56},{48,64},{56,72},{64,... | collective-permute-start | bytes 786440 | tf_op jit(solution)/shard_map/ppermute | solution.py:184
  4.4 1.9 %collective-permute-start.2 = (bf16[1024,128]{1,0:T(8,128)(2,1)S(1)}, bf16[1024,128]{1,0:T(8,128)(2,1)S(1)}, u32[]{:S(2)}, u32[]{:S(2)}) collective-permute-start(bf16[1024,128]{1,0:T(8,128)(2,1)S(1)} %get-tuple-element.13.refs_0_), channel_id=1, source_target_pairs={{0,8},{8,32},{16,24},{24,48},{32,40},{40,64},{48,56},{56,80},{64,7... | collective-permute-start | bytes 786440 | tf_op jit(solution)/shard_map/ppermute | solution.py:186
  6.4 9.6 %collective-permute-done.refs_2_ = bf16[1024,128]{1,0:T(8,128)(2,1)S(1)} collective-permute-done((bf16[1024,128]{1,0:T(8,128)(2,1)S(1)}, bf16[1024,128]{1,0:T(8,128)(2,1)S(1)}, u32[]{:S(2)}, u32[]{:S(2)}) %collective-permute-start) | collective-permute-done | bytes 262176 | tf_op jit(solution)/shard_map/ppermute | solution.py:184
  16.0 1.9 %collective-permute-start.1 = (bf16[1024,128]{1,0:T(8,128)(2,1)S(1)}, bf16[1024,128]{1,0:T(8,128)(2,1)S(1)}, u32[]{:S(2)}, u32[]{:S(2)}) collective-permute-start(bf16[1024,128]{1,0:T(8,128)(2,1)S(1)} %collective-permute-done.refs_2_), channel_id=1, source_target_pairs={{0,8},{8,0},{16,24},{24,16},{32,40},{40,32},{48,56},{56,48},{64,72... | collective-permute-start | bytes 786440 | tf_op jit(solution)/shard_map/ppermute | solution.py:187
  17.9 0.1 pad_add_fusion.where_ref
  18.0 2.9 %shard_map.46 = (bf16[512,512]{1,0:T(8,128)(2,1)S(1)}, f32[2048,128]{1,0:T(8,128)S(1)}, f32[2048,256]{1,0:T(8,128)S(1)}) custom-call(s32[2]{0:T(128)S(1)} %pad_add_fusion.where_ref, s32[2,128]{1,0:T(2,128)S(1)} %get-tuple-element.12.docs_ref, bf16[512,512]{1,0:T(8,128)(2,1)} %q_ref.1, bf16[1024,128]{1,0:T(8,128)(2,1)S(1)} %get-tuple-element.13.refs_0_), custom_call_target="tpu_custom_call" | custom-call | flops 1000000000 | bytes 1000000 | tf_op jit(solution)/shard_map/pallas_call | solution.py:131
  20.9 2.4 %shard_map.47 = (f32[2048,128]{1,0:T(8,128)S(1)}, f32[2048,256]{1,0:T(8,128)S(1)}) custom-call(s32[2]{0:T(128)S(1)} %pad_add_fusion.where_ref, s32[2,128]{1,0:T(2,128)S(1)} %get-tuple-element.12.docs_ref, bf16[512,512]{1,0:T(8,128)(2,1)S(1)} %get-tuple-element.14.q_ref, f32[2048,128]{1,0:T(8,128)S(1)} %get-tuple-element.15.refs_0_, ...), custom_call_target="tpu_custom_call" | custom-call | flops 1000000000 | bytes 1000000 | tf_op jit(solution)/shard_map/pallas_call | solution.py:131
  23.3 0.0 collective-permute-done.2.refs_3_
  23.3 0.0 collective-permute-done.1.refs_2_
  23.3 3.5 %shard_map.48 = bf16[512,512]{1,0:T(8,128)(2,1)S(1)} custom-call(s32[2]{0:T(128)S(1)} %pad_add_fusion.where_ref, s32[2,128]{1,0:T(2,128)S(1)} %get-tuple-element.12.docs_ref, bf16[512,512]{1,0:T(8,128)(2,1)S(1)} %get-tuple-element.14.q_ref, f32[2048,128]{1,0:T(8,128)S(1)} %get-tuple-element.17.refs_0_, f32[2048,256]{1,0:T(8,128)S(1)} %get-tuple-element.18.refs_1_, ...), custom_call_target="tpu_custom_call" | custom-call | flops 2000000000 | bytes 1000000 | tf_op jit(solution)/shard_map/pallas_call | solution.py:131
  26.8 25.1 %all_to_all.19 = bf16[8,64,512]{2,1,0:T(8,128)(2,1)S(1)} all-to-all(bf16[8,64,512]{2,1,0:T(8,128)(2,1)S(1)} %bitcast.6), channel_id=1, replica_groups=mesh['seq'=96,'head'=8] {'head'}, dimensions={0} | all-to-all | bytes 1048576 | tf_op jit(solution)/shard_map/all_to_all | solution.py:192
  51.9 0.8 %copy.6 = bf16[8,8,8,512]{3,2,0,1:T(8,128)(2,1)} copy(bf16[8,8,8,512]{3,2,1,0:T(8,128)(2,1)S(1)} %bitcast.7) | data formatting | bytes 1048576 | tf_op jit(solution)/shard_map/all_to_all | solution.py:192
Async XLA Ops:
  1.0 15.0 %collective-permute-start = (bf16[1024,128]{1,0:T(8,128)(2,1)S(1)}, bf16[1024,128]{1,0:T(8,128)(2,1)S(1)}, u32[]{:S(2)}, u32[]{:S(2)}) collective-permute-start(bf16[1024,128]{1,0:T(8,128)(2,1)S(1)} %get-tuple-element.13.refs_0_), channel_id=1, source_target_pairs={{0,16},{8,24},{16,32},{24,40},{32,48},{40,56},{48,64},{56,72},{64,... | collective-permute-start | bytes 786440 | tf_op jit(solution)/shard_map/ppermute | solution.py:184
  4.4 18.9 %collective-permute-start.2 = (bf16[1024,128]{1,0:T(8,128)(2,1)S(1)}, bf16[1024,128]{1,0:T(8,128)(2,1)S(1)}, u32[]{:S(2)}, u32[]{:S(2)}) collective-permute-start(bf16[1024,128]{1,0:T(8,128)(2,1)S(1)} %get-tuple-element.13.refs_0_), channel_id=1, source_target_pairs={{0,8},{8,32},{16,24},{24,48},{32,40},{40,64},{48,56},{56,80},{64,7... | collective-permute-start | bytes 786440 | tf_op jit(solution)/shard_map/ppermute | solution.py:186
  16.0 7.3 %collective-permute-start.1 = (bf16[1024,128]{1,0:T(8,128)(2,1)S(1)}, bf16[1024,128]{1,0:T(8,128)(2,1)S(1)}, u32[]{:S(2)}, u32[]{:S(2)}) collective-permute-start(bf16[1024,128]{1,0:T(8,128)(2,1)S(1)} %collective-permute-done.refs_2_), channel_id=1, source_target_pairs={{0,8},{8,0},{16,24},{24,16},{32,40},{40,32},{48,56},{56,48},{64,72... | collective-permute-start | bytes 786440 | tf_op jit(solution)/shard_map/ppermute | solution.py:187
where the time goes:
time: 53.2 us; the launch traced here: 52.7 us
  blocking collectives  25.1 us (47%)
  Pallas kernels  9.81 us (18%)
  waiting for transfers between devices  9.65 us (18%)
  starting transfers between devices  7.23 us (14%)
  local copies, waits for them, and re-layouts  0.84 us (2%)
    all_to_all x1, blocking collectives, per_device(): lax.all_to_all(merged, 'head', split_axis=0, concat_axis=1, tiled=True)  25.1 us
    ppermute x1, waiting for transfers between devices, per_device(): a = lax.ppermute(rows, 'seq', [(i, i + 2) for i in range(blocks - 2)])  9.64 us
    pallas_call x3, Pallas kernels, stage(): pl.pallas_call(functools.partial(attend, causal, start, last, backs), out...  8.81 us
    ppermute x1, starting transfers between devices, per_device(): a = lax.ppermute(rows, 'seq', [(i, i + 2) for i in range(blocks - 2)])  3.4 us
    ppermute x1, starting transfers between devices, per_device(): x = lax.ppermute(rows, 'seq', [(i, j) for i, j in hops if j < blocks])  1.92 us
    ppermute x1, starting transfers between devices, per_device(): s = lax.ppermute(a, 'seq', [(i, i ^ 1) for i in range(blocks)])  1.91 us
  transfers between devices with their start and end apart: 3, of which 1 were waited for; matrix products, arithmetic and copies ran while one was open for 0% of the time, Pallas kernels for 10%

commit v1 on v0

--- a/solution.py
+++ b/solution.py
@@ -34,13 +34,25 @@
         fetch.start()
     kw, vw = refs[-2:]
     outs = refs[:-2]
-    for i, (even_back, odd_back) in enumerate(backs):
-        rows = slice(i * T, (i + 1) * T)
-        base = first - (even_back + odd * (odd_back - even_back)) * T
-        kw[rows, :HD] = blocks[i][:T, :]
+
+    def put(slot, base, block):
+        rows = pl.ds(pl.multiple_of(slot * T, T), T)
+        kw[rows, :HD] = block[:T, :]
         kw[rows, HD:] = jnp.where(inside(docs_ref, base, T), 0.0, -FAR).astype(jnp.bfloat16)
-        vw[rows, :HD] = blocks[i][T:, :]
+        vw[rows, :HD] = block[T:, :]
         vw[rows, HD:] = jnp.ones((T, HD), jnp.bfloat16)
+
+    count = 0
+    if start:
+        put(0, first, blocks[0])
+    else:
+        begins = docs_ref[0:1, :]
+        reach = jnp.max(jnp.where(begins <= first, begins, 0).astype(jnp.float32))
+        for block, (even_back, odd_back) in zip(blocks, backs):
+            base = first - (even_back + odd * (odd_back - even_back)) * T
+            needed = reach < (base + T).astype(jnp.float32)
+            pl.when(needed)(functools.partial(put, count, base, block))
+            count = count + needed.astype(jnp.int32)
     below = None
     if causal:
         row = lax.broadcasted_iota(jnp.int32, (HEADS * QT, QT), 0) % QT
@@ -49,10 +61,10 @@
         jnp.where(inside(docs_ref, first + low, QT), 1.0, 0.0).astype(jnp.bfloat16) for low in range(0, T, QT)
     ]
 
-    def width(unit):
-        return unit[0] * QT + QT if causal else len(backs) * T
-
-    def score(unit):
+    def width(unit, n):
+        return unit[0] * QT + QT if causal else n * T
+
+    def score(unit, n):
         tile, head = unit
         rows = slice(tile * QT, tile * QT + QT)
         query = jnp.concatenate(
@@ -63,7 +75,7 @@
             0,
         )
         scores = lax.dot_general(
-            query, kw[: width(unit), :], (((1,), (1,)), ((), ())), preferred_element_type=jnp.float32
+            query, kw[: width(unit, n), :], (((1,), (1,)), ((), ())), preferred_element_type=jnp.float32
         )
         if causal:
             low = tile * QT
@@ -71,7 +83,7 @@
             scores = tail if low == 0 else jnp.concatenate([scores[:, :low], tail], 1)
         return scores
 
-    def mix(unit, scores):
+    def mix(unit, n, scores):
         tile, head = unit
         at = (tile * GROUP + head) * QT
         rows = slice(at, at + HEADS * QT)
@@ -82,30 +94,51 @@
             before = state[0][rows, :]
             largest = jnp.maximum(before, largest)
             shrink = jnp.exp2((before - largest) * SCALE)
-            weights = jnp.exp2((scores - jnp.concatenate([largest] * (width(unit) // HD), 1)) * SCALE)
+            weights = jnp.exp2((scores - jnp.concatenate([largest] * (width(unit, n) // HD), 1)) * SCALE)
             weights = weights.astype(jnp.bfloat16)
-        mixed = jnp.dot(weights, vw[: width(unit), :], preferred_element_type=jnp.float32)
+        mixed = jnp.dot(weights, vw[: width(unit, n), :], preferred_element_type=jnp.float32)
         top, total = mixed[:, :HD], mixed[:, HD:]
         if not start:
             top = top + state[1][rows, :HD] * shrink
             total = total + state[1][rows, HD:] * shrink
         if last:
-            result = (top / total).astype(jnp.bfloat16)
-            for i in range(HEADS):
-                columns = slice((head + i) * HD, (head + i + 1) * HD)
-                outs[0][tile * QT : tile * QT + QT, columns] = result[i * QT : (i + 1) * QT]
+            store(unit, top, total)
         else:
             outs[0][rows, :] = jnp.broadcast_to(largest, (HEADS * QT, HD))
             outs[1][rows, :HD] = top
             outs[1][rows, HD:] = total
 
+    def store(unit, top, total):
+        tile, head = unit
+        result = (top / total).astype(jnp.bfloat16)
+        for i in range(HEADS):
+            columns = slice((head + i) * HD, (head + i + 1) * HD)
+            outs[0][tile * QT : tile * QT + QT, columns] = result[i * QT : (i + 1) * QT]
+
     units = [(tile, head) for tile in range(T // QT) for head in range(0, GROUP, HEADS)]
+
+    def run(n):
+        ahead = score(units[0], n)
+        for i, unit in enumerate(units):
+            scores, ahead = ahead, score(units[i + 1], n) if i + 1 < len(units) else None
+            mix(unit, n, scores)
+
+    def rest():
+        if not last:
+            outs[0][...] = state[0][...]
+            outs[1][...] = state[1][...]
+            return
+        for tile, head in units:
+            rows = slice((tile * GROUP + head) * QT, (tile * GROUP + head + HEADS) * QT)
+            store((tile, head), state[1][rows, :HD], state[1][rows, HD:])
+
     if start:
         fetch.wait()
-    ahead = score(units[0])
-    for i, unit in enumerate(units):
-        scores, ahead = ahead, score(units[i + 1]) if i + 1 < len(units) else None
-        mix(unit, scores)
+        run(1)
+    else:
+        for n in range(1, len(blocks) + 1):
+            pl.when(count == n)(functools.partial(run, n))
+        pl.when(count == 0)(rest)
 
 
 STATE = [

time: 53.2 us -> 51.3 us (0.964)
  the two profiles are of different devices: /device:TPU:512 before, /device:TPU:257 now
where the time goes in v1:
time: 51.3 us; the launch traced here: 51.1 us
  blocking collectives  23.5 us (46%)
  starting transfers between devices  13.5 us (26%)
  Pallas kernels  9.06 us (18%)
  waiting for transfers between devices  4.06 us (8%)
  local copies, waits for them, and re-layouts  0.84 us (2%)
    all_to_all x1, blocking collectives, per_device(): lax.all_to_all(merged, 'head', split_axis=0, concat_axis=1, tiled=True)  23.5 us
    pallas_call x3, Pallas kernels, stage(): pl.pallas_call(functools.partial(attend, causal, start, last, backs), out...  8.06 us
    ppermute x1, starting transfers between devices, per_device(): x = lax.ppermute(rows, 'seq', [(i, j) for i, j in hops if j < blocks])  5.2 us
    ppermute x1, starting transfers between devices, per_device(): s = lax.ppermute(a, 'seq', [(i, i ^ 1) for i in range(blocks)])  5.16 us
    ppermute x1, waiting for transfers between devices, per_device(): a = lax.ppermute(rows, 'seq', [(i, i + 2) for i in range(blocks - 2)])  4.05 us
    ppermute x1, starting transfers between devices, per_device(): a = lax.ppermute(rows, 'seq', [(i, i + 2) for i in range(blocks - 2)])  3.12 us
  transfers between devices with their start and end apart: 3, of which 1 were waited for; matrix products, arithmetic and copies ran while one was open for 0% of the time, Pallas kernels for 11%

profile of v1, /device:TPU:257, one launch (start us, length us, event | category | flops | bytes accessed | tf_op | source)
XLA Modules:
  0.0 51.1 jit_solution(4124815801157210150)
XLA Ops:
  0.0 1.0 %pack.1 = (bf16[1024,128]{1,0:T(8,128)(2,1)S(1)}, s32[2,128]{1,0:T(2,128)S(1)}) custom-call(bf16[512,128]{1,0:T(8,128)(2,1)} %k_ref.1, bf16[512,128]{1,0:T(8,128)(2,1)} %v_ref.1, s32[96]{0:T(128)} %lengths_ref.1), custom_call_target="tpu_custom_call" | custom-call | tf_op jit(solution)/shard_map/pack/pallas_call | solution.py:203
  1.0 3.1 %collective-permute-start = (bf16[1024,128]{1,0:T(8,128)(2,1)S(1)}, bf16[1024,128]{1,0:T(8,128)(2,1)S(1)}, u32[]{:S(2)}, u32[]{:S(2)}) collective-permute-start(bf16[1024,128]{1,0:T(8,128)(2,1)S(1)} %get-tuple-element.13.refs_0_), channel_id=1, source_target_pairs={{0,16},{8,24},{16,32},{24,40},{32,48},{40,56},{48,64},{56,72},{64,... | collective-permute-start | bytes 786440 | tf_op jit(solution)/shard_map/ppermute | solution.py:217
  4.1 5.2 %collective-permute-start.2 = (bf16[1024,128]{1,0:T(8,128)(2,1)S(1)}, bf16[1024,128]{1,0:T(8,128)(2,1)S(1)}, u32[]{:S(2)}, u32[]{:S(2)}) collective-permute-start(bf16[1024,128]{1,0:T(8,128)(2,1)S(1)} %get-tuple-element.13.refs_0_), channel_id=1, source_target_pairs={{0,8},{8,32},{16,24},{24,48},{32,40},{40,64},{48,56},{56,80},{64,7... | collective-permute-start | bytes 786440 | tf_op jit(solution)/shard_map/ppermute | solution.py:219
  9.4 4.1 %collective-permute-done.refs_2_ = bf16[1024,128]{1,0:T(8,128)(2,1)S(1)} collective-permute-done((bf16[1024,128]{1,0:T(8,128)(2,1)S(1)}, bf16[1024,128]{1,0:T(8,128)(2,1)S(1)}, u32[]{:S(2)}, u32[]{:S(2)}) %collective-permute-start) | collective-permute-done | bytes 262176 | tf_op jit(solution)/shard_map/ppermute | solution.py:217
  13.4 5.2 %collective-permute-start.1 = (bf16[1024,128]{1,0:T(8,128)(2,1)S(1)}, bf16[1024,128]{1,0:T(8,128)(2,1)S(1)}, u32[]{:S(2)}, u32[]{:S(2)}) collective-permute-start(bf16[1024,128]{1,0:T(8,128)(2,1)S(1)} %collective-permute-done.refs_2_), channel_id=1, source_target_pairs={{0,8},{8,0},{16,24},{24,16},{32,40},{40,32},{48,56},{56,48},{64,72... | collective-permute-start | bytes 786440 | tf_op jit(solution)/shard_map/ppermute | solution.py:220
  18.6 0.1 pad_add_fusion.where_ref
  18.7 2.9 %shard_map.46 = (bf16[512,512]{1,0:T(8,128)(2,1)S(1)}, f32[2048,128]{1,0:T(8,128)S(1)}, f32[2048,256]{1,0:T(8,128)S(1)}) custom-call(s32[2]{0:T(128)S(1)} %pad_add_fusion.where_ref, s32[2,128]{1,0:T(2,128)S(1)} %get-tuple-element.12.docs_ref, bf16[512,512]{1,0:T(8,128)(2,1)} %q_ref.1, bf16[1024,128]{1,0:T(8,128)(2,1)S(1)} %get-tuple-element.13.refs_0_), custom_call_target="tpu_custom_call" | custom-call | flops 1000000000 | bytes 1000000 | tf_op jit(solution)/shard_map/pallas_call | solution.py:164
  21.5 2.6 %shard_map.47 = (f32[2048,128]{1,0:T(8,128)S(1)}, f32[2048,256]{1,0:T(8,128)S(1)}) custom-call(s32[2]{0:T(128)S(1)} %pad_add_fusion.where_ref, s32[2,128]{1,0:T(2,128)S(1)} %get-tuple-element.12.docs_ref, bf16[512,512]{1,0:T(8,128)(2,1)S(1)} %get-tuple-element.14.q_ref, f32[2048,128]{1,0:T(8,128)S(1)} %get-tuple-element.15.refs_0_, ...), custom_call_target="tpu_custom_call" | custom-call | flops 1000000000 | bytes 1000000 | tf_op jit(solution)/shard_map/pallas_call | solution.py:164
  24.1 0.0 collective-permute-done.2.refs_3_
  24.1 0.0 collective-permute-done.1.refs_2_
  24.1 2.6 %shard_map.48 = bf16[512,512]{1,0:T(8,128)(2,1)S(1)} custom-call(s32[2]{0:T(128)S(1)} %pad_add_fusion.where_ref, s32[2,128]{1,0:T(2,128)S(1)} %get-tuple-element.12.docs_ref, bf16[512,512]{1,0:T(8,128)(2,1)S(1)} %get-tuple-element.14.q_ref, f32[2048,128]{1,0:T(8,128)S(1)} %get-tuple-element.17.refs_0_, f32[2048,256]{1,0:T(8,128)S(1)} %get-tuple-element.18.refs_1_, ...), custom_call_target="tpu_custom_call" | custom-call | flops 2000000000 | bytes 1000000 | tf_op jit(solution)/shard_map/pallas_call | solution.py:164
  26.8 23.5 %all_to_all.19 = bf16[8,64,512]{2,1,0:T(8,128)(2,1)S(1)} all-to-all(bf16[8,64,512]{2,1,0:T(8,128)(2,1)S(1)} %bitcast.6), channel_id=1, replica_groups=mesh['seq'=96,'head'=8] {'head'}, dimensions={0} | all-to-all | bytes 1048576 | tf_op jit(solution)/shard_map/all_to_all | solution.py:225
  50.2 0.8 %copy.6 = bf16[8,8,8,512]{3,2,0,1:T(8,128)(2,1)} copy(bf16[8,8,8,512]{3,2,1,0:T(8,128)(2,1)S(1)} %bitcast.7) | data formatting | bytes 1048576 | tf_op jit(solution)/shard_map/all_to_all | solution.py:225
Async XLA Ops:
  1.0 12.4 %collective-permute-start = (bf16[1024,128]{1,0:T(8,128)(2,1)S(1)}, bf16[1024,128]{1,0:T(8,128)(2,1)S(1)}, u32[]{:S(2)}, u32[]{:S(2)}) collective-permute-start(bf16[1024,128]{1,0:T(8,128)(2,1)S(1)} %get-tuple-element.13.refs_0_), channel_id=1, source_target_pairs={{0,16},{8,24},{16,32},{24,40},{32,48},{40,56},{48,64},{56,72},{64,... | collective-permute-start | bytes 786440 | tf_op jit(solution)/shard_map/ppermute | solution.py:217
  4.1 20.0 %collective-permute-start.2 = (bf16[1024,128]{1,0:T(8,128)(2,1)S(1)}, bf16[1024,128]{1,0:T(8,128)(2,1)S(1)}, u32[]{:S(2)}, u32[]{:S(2)}) collective-permute-start(bf16[1024,128]{1,0:T(8,128)(2,1)S(1)} %get-tuple-element.13.refs_0_), channel_id=1, source_target_pairs={{0,8},{8,32},{16,24},{24,48},{32,40},{40,64},{48,56},{56,80},{64,7... | collective-permute-start | bytes 786440 | tf_op jit(solution)/shard_map/ppermute | solution.py:219
  13.4 10.7 %collective-permute-start.1 = (bf16[1024,128]{1,0:T(8,128)(2,1)S(1)}, bf16[1024,128]{1,0:T(8,128)(2,1)S(1)}, u32[]{:S(2)}, u32[]{:S(2)}) collective-permute-start(bf16[1024,128]{1,0:T(8,128)(2,1)S(1)} %collective-permute-done.refs_2_), channel_id=1, source_target_pairs={{0,8},{8,0},{16,24},{24,16},{32,40},{40,32},{48,56},{56,48},{64,72... | collective-permute-start | bytes 786440 | tf_op jit(solution)/shard_map/ppermute | solution.py:220

commit v2 on v1

--- a/solution.py
+++ b/solution.py
@@ -23,9 +23,10 @@
     return (position >= docs_ref[0:1, :]) & (position < docs_ref[1:2, :])
 
 
-def attend(causal, start, last, backs, where_ref, docs_ref, q_ref, *refs):
+def attend(causal, start, last, backs, docs_ref, q_ref, *refs):
     refs = list(refs)
-    first, odd = where_ref[0], where_ref[1]
+    place = lax.axis_index("seq")
+    first, odd = place * T, place % 2
     state = None if start else (refs.pop(0), refs.pop(0))
     blocks = [refs.pop(0) for _ in backs]
     if start:
@@ -152,7 +153,7 @@
     return pltpu.with_memory_space_constraint(x, pltpu.HBM)
 
 
-def stage(where, docs, queries, state, blocks, backs, causal=False, last=False):
+def stage(docs, queries, state, blocks, backs, causal=False, last=False):
     vmem = pl.BlockSpec(memory_space=pltpu.VMEM)
     start = not state
     out_shape = RESULT if last else STATE
@@ -164,7 +165,7 @@
     return pl.pallas_call(
         functools.partial(attend, causal, start, last, backs),
         out_shape=out_shape,
-        in_specs=[pl.BlockSpec(memory_space=pltpu.SMEM), vmem, pl.BlockSpec(memory_space=pltpu.HBM) if start else vmem]
+        in_specs=[vmem, pl.BlockSpec(memory_space=pltpu.HBM) if start else vmem]
         + [vmem] * len(args),
         out_specs=[vmem] * len(out_shape),
         scratch_shapes=scratch,
@@ -172,7 +173,7 @@
         cost_estimate=pl.CostEstimate(
             flops=10**9 * len(blocks), transcendentals=10**6 * len(blocks), bytes_accessed=10**6
         ),
-    )(where, docs, in_hbm(queries) if start else queries, *args)
+    )(docs, in_hbm(queries) if start else queries, *args)
 
 
 def pack_kernel(k_ref, v_ref, lengths_ref, rows_ref, docs_ref, lengths, sems):
@@ -212,16 +213,14 @@
 
 def per_device(queries, key_rows, value_rows, doc_lengths):
     blocks = lax.axis_size("seq")
-    block = lax.axis_index("seq")
     rows, docs = pack(key_rows, value_rows, doc_lengths)
     a = lax.ppermute(rows, "seq", [(i, i + 2) for i in range(blocks - 2)])
     hops = [(i, i + 1 if i % 2 == 0 else i + 3) for i in range(blocks)]
     x = lax.ppermute(rows, "seq", [(i, j) for i, j in hops if j < blocks])
     s = lax.ppermute(a, "seq", [(i, i ^ 1) for i in range(blocks)])
-    where = jnp.stack([block * T, block % 2]).astype(jnp.int32)
-    near, *state = stage(where, docs, queries, (), (rows,), ((0, 0),), causal=True)
-    state = stage(where, docs, near, state, (a,), ((2, 2),))
-    (merged,) = stage(where, docs, near, state, (s, x), ((1, 3), (3, 1)), last=True)
+    near, *state = stage(docs, queries, (), (rows,), ((0, 0),), causal=True)
+    state = stage(docs, near, state, (a,), ((2, 2),))
+    (merged,) = stage(docs, near, state, (s, x), ((1, 3), (3, 1)), last=True)
     return lax.all_to_all(merged, "head", split_axis=0, concat_axis=1, tiled=True)
 
 

time: 51.3 us -> 49.7 us (0.969)
  Pallas kernels: 9.06 us -> 7.48 us
    pallas_call x3, Pallas kernels: 8.06 us -> 6.48 us  [stage(): pl.pallas_call(functools.partial(attend, causal, start, last, backs), out...]
  transfers between devices with their start and end apart: 3 -> 3, of which waited for: 1 -> 1; matrix products, arithmetic and copies ran while one was open for 0% -> 0% of each run, Pallas kernels for 11% -> 9%
where the time goes in v2:
time: 49.7 us; the launch traced here: 49.4 us
  blocking collectives  23.5 us (47%)
  starting transfers between devices  13.5 us (27%)
  Pallas kernels  7.48 us (15%)
  waiting for transfers between devices  4.08 us (8%)
  local copies, waits for them, and re-layouts  0.84 us (2%)
    all_to_all x1, blocking collectives, per_device(): lax.all_to_all(merged, 'head', split_axis=0, concat_axis=1, tiled=True)  23.5 us
    pallas_call x3, Pallas kernels, stage(): pl.pallas_call(functools.partial(attend, causal, start, last, backs), out...  6.48 us
    ppermute x1, starting transfers between devices, per_device(): x = lax.ppermute(rows, 'seq', [(i, j) for i, j in hops if j < blocks])  5.2 us
    ppermute x1, starting transfers between devices, per_device(): s = lax.ppermute(a, 'seq', [(i, i ^ 1) for i in range(blocks)])  5.16 us
    ppermute x1, waiting for transfers between devices, per_device(): a = lax.ppermute(rows, 'seq', [(i, i + 2) for i in range(blocks - 2)])  4.07 us
    ppermute x1, starting transfers between devices, per_device(): a = lax.ppermute(rows, 'seq', [(i, i + 2) for i in range(blocks - 2)])  3.12 us
  transfers between devices with their start and end apart: 3, of which 1 were waited for; matrix products, arithmetic and copies ran while one was open for 0% of the time, Pallas kernels for 9%

profile of v2, /device:TPU:257, one launch (start us, length us, event | category | flops | bytes accessed | tf_op | source)
XLA Modules:
  0.0 49.4 jit_solution(2474759330361936955)
XLA Ops:
  0.0 1.0 %pack.1 = (bf16[1024,128]{1,0:T(8,128)(2,1)S(1)}, s32[2,128]{1,0:T(2,128)S(1)}) custom-call(bf16[512,128]{1,0:T(8,128)(2,1)} %k_ref.1, bf16[512,128]{1,0:T(8,128)(2,1)} %v_ref.1, s32[96]{0:T(128)} %lengths_ref.1), custom_call_target="tpu_custom_call" | custom-call | tf_op jit(solution)/shard_map/pack/pallas_call | solution.py:204
  1.0 3.1 %collective-permute-start = (bf16[1024,128]{1,0:T(8,128)(2,1)S(1)}, bf16[1024,128]{1,0:T(8,128)(2,1)S(1)}, u32[]{:S(2)}, u32[]{:S(2)}) collective-permute-start(bf16[1024,128]{1,0:T(8,128)(2,1)S(1)} %get-tuple-element.13.refs_0_), channel_id=1, source_target_pairs={{0,16},{8,24},{16,32},{24,40},{32,48},{40,56},{48,64},{56,72},{64,... | collective-permute-start | bytes 786440 | tf_op jit(solution)/shard_map/ppermute | solution.py:217
  4.1 5.2 %collective-permute-start.2 = (bf16[1024,128]{1,0:T(8,128)(2,1)S(1)}, bf16[1024,128]{1,0:T(8,128)(2,1)S(1)}, u32[]{:S(2)}, u32[]{:S(2)}) collective-permute-start(bf16[1024,128]{1,0:T(8,128)(2,1)S(1)} %get-tuple-element.13.refs_0_), channel_id=1, source_target_pairs={{0,8},{8,32},{16,24},{24,48},{32,40},{40,64},{48,56},{56,80},{64,7... | collective-permute-start | bytes 786440 | tf_op jit(solution)/shard_map/ppermute | solution.py:219
  9.3 4.1 %collective-permute-done.refs_2_ = bf16[1024,128]{1,0:T(8,128)(2,1)S(1)} collective-permute-done((bf16[1024,128]{1,0:T(8,128)(2,1)S(1)}, bf16[1024,128]{1,0:T(8,128)(2,1)S(1)}, u32[]{:S(2)}, u32[]{:S(2)}) %collective-permute-start) | collective-permute-done | bytes 262176 | tf_op jit(solution)/shard_map/ppermute | solution.py:217
  13.4 5.2 %collective-permute-start.1 = (bf16[1024,128]{1,0:T(8,128)(2,1)S(1)}, bf16[1024,128]{1,0:T(8,128)(2,1)S(1)}, u32[]{:S(2)}, u32[]{:S(2)}) collective-permute-start(bf16[1024,128]{1,0:T(8,128)(2,1)S(1)} %collective-permute-done.refs_2_), channel_id=1, source_target_pairs={{0,8},{8,0},{16,24},{24,16},{32,40},{40,32},{48,56},{56,48},{64,72... | collective-permute-start | bytes 786440 | tf_op jit(solution)/shard_map/ppermute | solution.py:220
  18.6 2.3 %shard_map.46 = (bf16[512,512]{1,0:T(8,128)(2,1)S(1)}, f32[2048,128]{1,0:T(8,128)S(1)}, f32[2048,256]{1,0:T(8,128)S(1)}) custom-call(s32[2,128]{1,0:T(2,128)S(1)} %get-tuple-element.12.docs_ref, bf16[512,512]{1,0:T(8,128)(2,1)} %q_ref.1, bf16[1024,128]{1,0:T(8,128)(2,1)S(1)} %get-tuple-element.13.refs_0_), custom_call_target="tpu_custom_call" | custom-call | flops 1000000000 | bytes 1000000 | tf_op jit(solution)/shard_map/pallas_call | solution.py:165
  20.9 2.0 %shard_map.47 = (f32[2048,128]{1,0:T(8,128)S(1)}, f32[2048,256]{1,0:T(8,128)S(1)}) custom-call(s32[2,128]{1,0:T(2,128)S(1)} %get-tuple-element.12.docs_ref, bf16[512,512]{1,0:T(8,128)(2,1)S(1)} %get-tuple-element.14.q_ref, f32[2048,128]{1,0:T(8,128)S(1)} %get-tuple-element.15.refs_0_, f32[2048,256]{1,0:T(8,128)S(1)} %get-tuple-element.16.refs_1_, ...), custom_call_target="tpu_custom_call" | custom-call | flops 1000000000 | bytes 1000000 | tf_op jit(solution)/shard_map/pallas_call | solution.py:165
  23.0 0.0 collective-permute-done.2.refs_3_
  23.0 0.0 collective-permute-done.1.refs_2_
  23.0 2.1 %shard_map.48 = bf16[512,512]{1,0:T(8,128)(2,1)S(1)} custom-call(s32[2,128]{1,0:T(2,128)S(1)} %get-tuple-element.12.docs_ref, bf16[512,512]{1,0:T(8,128)(2,1)S(1)} %get-tuple-element.14.q_ref, f32[2048,128]{1,0:T(8,128)S(1)} %get-tuple-element.17.refs_0_, f32[2048,256]{1,0:T(8,128)S(1)} %get-tuple-element.18.refs_1_, ...), custom_call_target="tpu_custom_call" | custom-call | flops 2000000000 | bytes 1000000 | tf_op jit(solution)/shard_map/pallas_call | solution.py:165
  25.1 23.5 %all_to_all.19 = bf16[8,64,512]{2,1,0:T(8,128)(2,1)S(1)} all-to-all(bf16[8,64,512]{2,1,0:T(8,128)(2,1)S(1)} %bitcast.4), channel_id=1, replica_groups=mesh['seq'=96,'head'=8] {'head'}, dimensions={0} | all-to-all | bytes 1048576 | tf_op jit(solution)/shard_map/all_to_all | solution.py:224
  48.6 0.8 %copy.6 = bf16[8,8,8,512]{3,2,0,1:T(8,128)(2,1)} copy(bf16[8,8,8,512]{3,2,1,0:T(8,128)(2,1)S(1)} %bitcast.5) | data formatting | bytes 1048576 | tf_op jit(solution)/shard_map/all_to_all | solution.py:224
Async XLA Ops:
  1.0 12.4 %collective-permute-start = (bf16[1024,128]{1,0:T(8,128)(2,1)S(1)}, bf16[1024,128]{1,0:T(8,128)(2,1)S(1)}, u32[]{:S(2)}, u32[]{:S(2)}) collective-permute-start(bf16[1024,128]{1,0:T(8,128)(2,1)S(1)} %get-tuple-element.13.refs_0_), channel_id=1, source_target_pairs={{0,16},{8,24},{16,32},{24,40},{32,48},{40,56},{48,64},{56,72},{64,... | collective-permute-start | bytes 786440 | tf_op jit(solution)/shard_map/ppermute | solution.py:217
  4.1 18.8 %collective-permute-start.2 = (bf16[1024,128]{1,0:T(8,128)(2,1)S(1)}, bf16[1024,128]{1,0:T(8,128)(2,1)S(1)}, u32[]{:S(2)}, u32[]{:S(2)}) collective-permute-start(bf16[1024,128]{1,0:T(8,128)(2,1)S(1)} %get-tuple-element.13.refs_0_), channel_id=1, source_target_pairs={{0,8},{8,32},{16,24},{24,48},{32,40},{40,64},{48,56},{56,80},{64,7... | collective-permute-start | bytes 786440 | tf_op jit(solution)/shard_map/ppermute | solution.py:219
  13.4 9.6 %collective-permute-start.1 = (bf16[1024,128]{1,0:T(8,128)(2,1)S(1)}, bf16[1024,128]{1,0:T(8,128)(2,1)S(1)}, u32[]{:S(2)}, u32[]{:S(2)}) collective-permute-start(bf16[1024,128]{1,0:T(8,128)(2,1)S(1)} %collective-permute-done.refs_2_), channel_id=1, source_target_pairs={{0,8},{8,0},{16,24},{24,16},{32,40},{40,32},{48,56},{56,48},{64,72... | collective-permute-start | bytes 786440 | tf_op jit(solution)/shard_map/ppermute | solution.py:220

commit v3 on v2

--- a/solution.py
+++ b/solution.py
@@ -23,6 +23,19 @@
     return (position >= docs_ref[0:1, :]) & (position < docs_ref[1:2, :])
 
 
+def tabulate(lengths, docs_ref):
+    lane = lax.broadcasted_iota(jnp.int32, (1, LANES), 1)
+    begins = jnp.full((1, LANES), 1 << 30, jnp.int32)
+    ends = begins
+    reached = jnp.int32(0)
+    for i in range(lengths.shape[0]):
+        begins = jnp.where(lane == i, reached, begins)
+        reached = reached + lengths[i]
+        ends = jnp.where(lane == i, reached, ends)
+    docs_ref[0:1, :] = begins
+    docs_ref[1:2, :] = ends
+
+
 def attend(causal, start, last, backs, docs_ref, q_ref, *refs):
     refs = list(refs)
     place = lax.axis_index("seq")
@@ -30,9 +43,15 @@
     state = None if start else (refs.pop(0), refs.pop(0))
     blocks = [refs.pop(0) for _ in backs]
     if start:
-        sem, q_hbm, q_ref = refs.pop(), q_ref, refs.pop(0)
-        fetch = pltpu.make_async_copy(q_hbm, q_ref, sem)
+        sems, lengths = refs.pop(), refs.pop()
+        q_hbm, q_ref = q_ref, refs.pop(0)
+        lengths_hbm, docs_ref = docs_ref, refs.pop(0)
+        fetch = pltpu.make_async_copy(q_hbm, q_ref, sems.at[0])
+        count_in = pltpu.make_async_copy(lengths_hbm, lengths, sems.at[1])
+        count_in.start()
         fetch.start()
+        count_in.wait()
+        tabulate(lengths, docs_ref)
     kw, vw = refs[-2:]
     outs = refs[:-2]
 
@@ -159,66 +178,56 @@
     out_shape = RESULT if last else STATE
     scratch = [pltpu.VMEM((len(blocks) * T, 2 * HD), jnp.bfloat16)] * 2
     if start:
-        out_shape = [jax.ShapeDtypeStruct(queries.shape, queries.dtype)] + out_shape
-        scratch.append(pltpu.SemaphoreType.DMA(()))
+        out_shape = [
+            jax.ShapeDtypeStruct(queries.shape, queries.dtype),
+            pltpu.VMEM((2, LANES), jnp.int32),
+        ] + out_shape
+        scratch += [pltpu.SMEM(docs.shape, jnp.int32), pltpu.SemaphoreType.DMA((2,))]
     args = (*state, *blocks)
     return pl.pallas_call(
         functools.partial(attend, causal, start, last, backs),
         out_shape=out_shape,
-        in_specs=[vmem, pl.BlockSpec(memory_space=pltpu.HBM) if start else vmem]
-        + [vmem] * len(args),
+        in_specs=[pl.BlockSpec(memory_space=pltpu.HBM) if start else vmem] * 2 + [vmem] * len(args),
         out_specs=[vmem] * len(out_shape),
         scratch_shapes=scratch,
         compiler_params=pltpu.CompilerParams(vmem_limit_bytes=28 << 20),
         cost_estimate=pl.CostEstimate(
             flops=10**9 * len(blocks), transcendentals=10**6 * len(blocks), bytes_accessed=10**6
         ),
-    )(docs, in_hbm(queries) if start else queries, *args)
-
-
-def pack_kernel(k_ref, v_ref, lengths_ref, rows_ref, docs_ref, lengths, sems):
+    )(*((in_hbm(docs), in_hbm(queries)) if start else (docs, queries)), *args)
+
+
+def pack_kernel(k_ref, v_ref, rows_ref, sems):
     copies = [
-        pltpu.make_async_copy(lengths_ref, lengths, sems.at[0]),
-        pltpu.make_async_copy(k_ref, rows_ref.at[:T, :], sems.at[1]),
-        pltpu.make_async_copy(v_ref, rows_ref.at[T:, :], sems.at[2]),
+        pltpu.make_async_copy(k_ref, rows_ref.at[:T, :], sems.at[0]),
+        pltpu.make_async_copy(v_ref, rows_ref.at[T:, :], sems.at[1]),
     ]
     for copy in copies:
         copy.start()
-    copies[0].wait()
-    lane = lax.broadcasted_iota(jnp.int32, (1, LANES), 1)
-    begins = jnp.full((1, LANES), 1 << 30, jnp.int32)
-    ends = begins
-    reached = jnp.int32(0)
-    for i in range(lengths.shape[0]):
-        begins = jnp.where(lane == i, reached, begins)
-        reached = reached + lengths[i]
-        ends = jnp.where(lane == i, reached, ends)
-    docs_ref[0:1, :] = begins
-    docs_ref[1:2, :] = ends
-    copies[1].wait()
-    copies[2].wait()
-
-
-def pack(keys, values, doc_lengths):
+    for copy in copies:
+        copy.wait()
+
+
+def pack(keys, values):
     vmem = pl.BlockSpec(memory_space=pltpu.VMEM)
     return pl.pallas_call(
         pack_kernel,
-        out_shape=[pltpu.VMEM((2 * T, HD), jnp.bfloat16), pltpu.VMEM((2, LANES), jnp.int32)],
-        in_specs=[pl.BlockSpec(memory_space=pltpu.HBM)] * 3,
-        out_specs=[vmem, vmem],
-        scratch_shapes=[pltpu.SMEM(doc_lengths.shape, jnp.int32), pltpu.SemaphoreType.DMA((3,))],
+        out_shape=pltpu.VMEM((2 * T, HD), jnp.bfloat16),
+        in_specs=[pl.BlockSpec(memory_space=pltpu.HBM)] * 2,
+        out_specs=vmem,
+        scratch_shapes=[pltpu.SemaphoreType.DMA((2,))],
         name="pack",
-    )(*(in_hbm(x) for x in (keys, values, doc_lengths)))
+    )(in_hbm(keys), in_hbm(values))
 
 
 def per_device(queries, key_rows, value_rows, doc_lengths):
     blocks = lax.axis_size("seq")
-    rows, docs = pack(key_rows, value_rows, doc_lengths)
+    rows = pack(key_rows, value_rows)
     a = lax.ppermute(rows, "seq", [(i, i + 2) for i in range(blocks - 2)])
     hops = [(i, i + 1 if i % 2 == 0 else i + 3) for i in range(blocks)]
     x = lax.ppermute(rows, "seq", [(i, j) for i, j in hops if j < blocks])
     s = lax.ppermute(a, "seq", [(i, i ^ 1) for i in range(blocks)])
-    near, *state = stage(docs, queries, (), (rows,), ((0, 0),), causal=True)
+    near, docs, *state = stage(doc_lengths, queries, (), (rows,), ((0, 0),), causal=True)
     state = stage(docs, near, state, (a,), ((2, 2),))
     (merged,) = stage(docs, near, state, (s, x), ((1, 3), (3, 1)), last=True)
     return lax.all_to_all(merged, "head", split_axis=0, concat_axis=1, tiled=True)

time: 49.7 us -> 49.6 us (level)
  no operation moved by 1% of the time
where the time goes in v3:
time: 49.6 us; the launch traced here: 49.4 us
  blocking collectives  23.5 us (47%)
  starting transfers between devices  13.5 us (27%)
  Pallas kernels  7.47 us (15%)
  waiting for transfers between devices  4.08 us (8%)
  local copies, waits for them, and re-layouts  0.84 us (2%)
    all_to_all x1, blocking collectives, per_device(): lax.all_to_all(merged, 'head', split_axis=0, concat_axis=1, tiled=True)  23.5 us
    pallas_call x3, Pallas kernels, stage(): pl.pallas_call(functools.partial(attend, causal, start, last, backs), out...  6.49 us
    ppermute x1, starting transfers between devices, per_device(): x = lax.ppermute(rows, 'seq', [(i, j) for i, j in hops if j < blocks])  5.2 us
    ppermute x1, starting transfers between devices, per_device(): s = lax.ppermute(a, 'seq', [(i, i ^ 1) for i in range(blocks)])  5.16 us
    ppermute x1, waiting for transfers between devices, per_device(): a = lax.ppermute(rows, 'seq', [(i, i + 2) for i in range(blocks - 2)])  4.07 us
    ppermute x1, starting transfers between devices, per_device(): a = lax.ppermute(rows, 'seq', [(i, i + 2) for i in range(blocks - 2)])  3.12 us
  transfers between devices with their start and end apart: 3, of which 1 were waited for; matrix products, arithmetic and copies ran while one was open for 0% of the time, Pallas kernels for 9%

profile of v3, /device:TPU:257, one launch (start us, length us, event | category | flops | bytes accessed | tf_op | source)
XLA Modules:
  0.0 49.4 jit_solution(6989695629786033576)
XLA Ops:
  0.0 1.0 %pack.1.refs_0_ = bf16[1024,128]{1,0:T(8,128)(2,1)S(1)} custom-call(bf16[512,128]{1,0:T(8,128)(2,1)} %k_ref.1, bf16[512,128]{1,0:T(8,128)(2,1)} %v_ref.1), custom_call_target="tpu_custom_call" | custom-call | tf_op jit(solution)/shard_map/pack/pallas_call | solution.py:213
  1.0 3.1 %collective-permute-start = (bf16[1024,128]{1,0:T(8,128)(2,1)S(1)}, bf16[1024,128]{1,0:T(8,128)(2,1)S(1)}, u32[]{:S(2)}, u32[]{:S(2)}) collective-permute-start(bf16[1024,128]{1,0:T(8,128)(2,1)S(1)} %pack.1.refs_0_), channel_id=1, source_target_pairs={{0,16},{8,24},{16,32},{24,40},{32,48},{40,56},{48,64},{56,72},{64,... | collective-permute-start | bytes 786440 | tf_op jit(solution)/shard_map/ppermute | solution.py:226
  4.1 5.2 %collective-permute-start.2 = (bf16[1024,128]{1,0:T(8,128)(2,1)S(1)}, bf16[1024,128]{1,0:T(8,128)(2,1)S(1)}, u32[]{:S(2)}, u32[]{:S(2)}) collective-permute-start(bf16[1024,128]{1,0:T(8,128)(2,1)S(1)} %pack.1.refs_0_), channel_id=1, source_target_pairs={{0,8},{8,32},{16,24},{24,48},{32,40},{40,64},{48,56},{56,80},{64,7... | collective-permute-start | bytes 786440 | tf_op jit(solution)/shard_map/ppermute | solution.py:228
  9.3 4.1 %collective-permute-done.refs_2_ = bf16[1024,128]{1,0:T(8,128)(2,1)S(1)} collective-permute-done((bf16[1024,128]{1,0:T(8,128)(2,1)S(1)}, bf16[1024,128]{1,0:T(8,128)(2,1)S(1)}, u32[]{:S(2)}, u32[]{:S(2)}) %collective-permute-start) | collective-permute-done | bytes 262176 | tf_op jit(solution)/shard_map/ppermute | solution.py:226
  13.4 5.2 %collective-permute-start.1 = (bf16[1024,128]{1,0:T(8,128)(2,1)S(1)}, bf16[1024,128]{1,0:T(8,128)(2,1)S(1)}, u32[]{:S(2)}, u32[]{:S(2)}) collective-permute-start(bf16[1024,128]{1,0:T(8,128)(2,1)S(1)} %collective-permute-done.refs_2_), channel_id=1, source_target_pairs={{0,8},{8,0},{16,24},{24,16},{32,40},{40,32},{48,56},{56,48},{64,72... | collective-permute-start | bytes 786440 | tf_op jit(solution)/shard_map/ppermute | solution.py:229
  18.6 2.3 %shard_map.46 = (bf16[512,512]{1,0:T(8,128)(2,1)S(1)}, s32[2,128]{1,0:T(2,128)S(1)}, f32[2048,128]{1,0:T(8,128)S(1)}, f32[2048,256]{1,0:T(8,128)S(1)}) custom-call(s32[96]{0:T(128)} %docs_ref.1, bf16[512,512]{1,0:T(8,128)(2,1)} %q_ref.1, bf16[1024,128]{1,0:T(8,128)(2,1)S(1)} %pack.1.refs_0_), custom_call_target="tpu_custom_call" | custom-call | flops 1000000000 | bytes 1000000 | tf_op jit(solution)/shard_map/pallas_call | solution.py:187
  20.9 2.0 %shard_map.47 = (f32[2048,128]{1,0:T(8,128)S(1)}, f32[2048,256]{1,0:T(8,128)S(1)}) custom-call(s32[2,128]{1,0:T(2,128)S(1)} %get-tuple-element.11.docs_ref, bf16[512,512]{1,0:T(8,128)(2,1)S(1)} %get-tuple-element.12.q_ref, f32[2048,128]{1,0:T(8,128)S(1)} %get-tuple-element.13.refs_0_, f32[2048,256]{1,0:T(8,128)S(1)} %get-tuple-element.14.refs_1_, ...), custom_call_target="tpu_custom_call" | custom-call | flops 1000000000 | bytes 1000000 | tf_op jit(solution)/shard_map/pallas_call | solution.py:187
  23.0 0.0 collective-permute-done.2.refs_3_
  23.0 0.0 collective-permute-done.1.refs_2_
  23.0 2.1 %shard_map.48 = bf16[512,512]{1,0:T(8,128)(2,1)S(1)} custom-call(s32[2,128]{1,0:T(2,128)S(1)} %get-tuple-element.11.docs_ref, bf16[512,512]{1,0:T(8,128)(2,1)S(1)} %get-tuple-element.12.q_ref, f32[2048,128]{1,0:T(8,128)S(1)} %get-tuple-element.15.refs_0_, f32[2048,256]{1,0:T(8,128)S(1)} %get-tuple-element.16.refs_1_, ...), custom_call_target="tpu_custom_call" | custom-call | flops 2000000000 | bytes 1000000 | tf_op jit(solution)/shard_map/pallas_call | solution.py:187
  25.1 23.5 %all_to_all.19 = bf16[8,64,512]{2,1,0:T(8,128)(2,1)S(1)} all-to-all(bf16[8,64,512]{2,1,0:T(8,128)(2,1)S(1)} %bitcast.4), channel_id=1, replica_groups=mesh['seq'=96,'head'=8] {'head'}, dimensions={0} | all-to-all | bytes 1048576 | tf_op jit(solution)/shard_map/all_to_all | solution.py:233
  48.6 0.8 %copy.6 = bf16[8,8,8,512]{3,2,0,1:T(8,128)(2,1)} copy(bf16[8,8,8,512]{3,2,1,0:T(8,128)(2,1)S(1)} %bitcast.5) | data formatting | bytes 1048576 | tf_op jit(solution)/shard_map/all_to_all | solution.py:233
Async XLA Ops:
  1.0 12.4 %collective-permute-start = (bf16[1024,128]{1,0:T(8,128)(2,1)S(1)}, bf16[1024,128]{1,0:T(8,128)(2,1)S(1)}, u32[]{:S(2)}, u32[]{:S(2)}) collective-permute-start(bf16[1024,128]{1,0:T(8,128)(2,1)S(1)} %pack.1.refs_0_), channel_id=1, source_target_pairs={{0,16},{8,24},{16,32},{24,40},{32,48},{40,56},{48,64},{56,72},{64,... | collective-permute-start | bytes 786440 | tf_op jit(solution)/shard_map/ppermute | solution.py:226
  4.1 18.8 %collective-permute-start.2 = (bf16[1024,128]{1,0:T(8,128)(2,1)S(1)}, bf16[1024,128]{1,0:T(8,128)(2,1)S(1)}, u32[]{:S(2)}, u32[]{:S(2)}) collective-permute-start(bf16[1024,128]{1,0:T(8,128)(2,1)S(1)} %pack.1.refs_0_), channel_id=1, source_target_pairs={{0,8},{8,32},{16,24},{24,48},{32,40},{40,64},{48,56},{56,80},{64,7... | collective-permute-start | bytes 786440 | tf_op jit(solution)/shard_map/ppermute | solution.py:228
  13.4 9.6 %collective-permute-start.1 = (bf16[1024,128]{1,0:T(8,128)(2,1)S(1)}, bf16[1024,128]{1,0:T(8,128)(2,1)S(1)}, u32[]{:S(2)}, u32[]{:S(2)}) collective-permute-start(bf16[1024,128]{1,0:T(8,128)(2,1)S(1)} %collective-permute-done.refs_2_), channel_id=1, source_target_pairs={{0,8},{8,0},{16,24},{24,16},{32,40},{40,32},{48,56},{56,48},{64,72... | collective-permute-start | bytes 786440 | tf_op jit(solution)/shard_map/ppermute | solution.py:229
